TPU v7x, 16 devices: a whole 2x2x2 slice. The times are simulated.
16 devices in a mesh: pc: 2 (over z), pr: 8 (over y, x, core).
Axes of the slice: x: 2, y: 2, z: 2, core: 2. Of those that a mesh axis runs over, the one named last changes fastest.
Arguments:
- a_panels: float32 [32768, 2, 64], P('pr', 'pc')
- a_trail: float32 [32768, 3968], P('pr', 'pc')
Outputs:
- output 1: float32 [32768, 2, 64], P('pr', 'pc')
- output 2: float32 [32768, 3968], P('pr', 'pc')
- output 3: float32 [128], replicated
All inputs are finite; a program needn't handle non-finite values.
Results may differ from a plain program's by a relative error of at most 0.001.
Values sent between devices are 32-bit elements.
A program may use at most 1 GiB of HBM per device.

v0:
```python
import jax
import jax.numpy as jnp
from jax import lax
from jax.sharding import PartitionSpec as P, NamedSharding

FULL_PRECISION = lax.Precision.HIGHEST


def mat_prod(form, left, right):
    return jnp.einsum(form, left, right, precision=FULL_PRECISION, preferred_element_type=jnp.float32)


def factor_panel(panel_blk, row_ids, first_row):
    blk_width = panel_blk.shape[1]
    col_ids = jnp.arange(blk_width)

    def column_step(j, carry):
        fac_panel, tau_vec = carry
        diag_row = first_row + j
        column = lax.dynamic_slice_in_dim(fac_panel, j, 1, axis=1)[:, 0]
        below_diag = row_ids > diag_row
        at_diag = row_ids == diag_row
        local_stats = jnp.stack([jnp.sum(jnp.where(row_ids >= diag_row, column * column, 0.0)), jnp.sum(jnp.where(at_diag, column, 0.0))])
        sum_stats = lax.psum(local_stats, 'pr')
        diag_val = sum_stats[1]
        col_norm = jnp.sqrt(sum_stats[0])
        beta_val = jnp.where(diag_val >= 0.0, -col_norm, col_norm)
        tau_j = (beta_val - diag_val) / beta_val
        house_vec = jnp.where(below_diag, column / (diag_val - beta_val), jnp.where(at_diag, 1.0, 0.0))
        proj_row = lax.psum(mat_prod('r,rc->c', house_vec, fac_panel), 'pr')
        proj_row = jnp.where(col_ids > j, tau_j * proj_row, 0.0)
        fac_panel = fac_panel - house_vec[:, None] * proj_row[None, :]
        new_col = jnp.where(below_diag, house_vec, jnp.where(at_diag, beta_val, column))
        fac_panel = jnp.where(col_ids[None, :] == j, new_col[:, None], fac_panel)
        tau_vec = jnp.where(col_ids == j, tau_j, tau_vec)
        return fac_panel, tau_vec

    return lax.fori_loop(0, blk_width, column_step, (panel_blk, jnp.zeros((blk_width,), panel_blk.dtype)))


def unit_lower(fac_panel, row_ids, first_row):
    diag_rows = first_row + jnp.arange(fac_panel.shape[1])
    return jnp.where(row_ids[:, None] > diag_rows[None, :], fac_panel, jnp.where(row_ids[:, None] == diag_rows[None, :], 1.0, 0.0))


def build_t(gram_mat, tau_vec):
    blk_width = tau_vec.shape[0]
    col_ids = jnp.arange(blk_width)

    def t_step(j, t_mat):
        g_col = jnp.where(col_ids < j, lax.dynamic_slice_in_dim(gram_mat, j, 1, axis=1)[:, 0], 0.0)
        tau_j = jnp.sum(jnp.where(col_ids == j, tau_vec, 0.0))
        new_col = -tau_j * mat_prod('ij,j->i', t_mat, g_col)
        new_col = jnp.where(col_ids == j, tau_j, new_col)
        return jnp.where(col_ids[None, :] == j, new_col[:, None], t_mat)

    return lax.fori_loop(0, blk_width, t_step, jnp.zeros((blk_width, blk_width), gram_mat.dtype))


def solution(mesh):
    proc_cols = mesh.shape['pc']

    def local_run(panels_loc, trail_loc):
        n_rows, per_col, blk_width = panels_loc.shape
        col_idx = lax.axis_index('pc')
        row_ids = lax.axis_index('pr') * n_rows + jnp.arange(n_rows)
        panel_cols = per_col * blk_width
        work_mat = jnp.concatenate([panels_loc.reshape(n_rows, panel_cols), trail_loc], axis=1)
        tau_parts = []
        for k in range(per_col * proc_cols):
            owner_col = k % proc_cols
            col_lo = (k // proc_cols) * blk_width
            first_row = k * blk_width
            fac_panel, tau_vec = factor_panel(work_mat[:, col_lo:col_lo + blk_width], row_ids, first_row)
            v_mat = unit_lower(fac_panel, row_ids, first_row)
            t_mat = build_t(lax.psum(mat_prod('rb,rc->bc', v_mat, v_mat), 'pr'), tau_vec)
            is_owner = col_idx == owner_col
            packed = jnp.concatenate([v_mat, t_mat, tau_vec[None, :]], axis=0)
            packed = lax.psum(jnp.where(is_owner, packed, 0.0), 'pc')
            v_mat = packed[:n_rows]
            t_mat = packed[n_rows:n_rows + blk_width]
            tau_vec = packed[n_rows + blk_width]
            tail_cols = work_mat[:, col_lo:]
            inner_prod = lax.psum(mat_prod('rb,rc->bc', v_mat, tail_cols), 'pr')
            inner_prod = mat_prod('bd,bc->dc', t_mat, inner_prod)
            tail_ids = jnp.arange(tail_cols.shape[1])
            inner_prod = jnp.where((tail_ids >= blk_width) | (col_idx > owner_col), inner_prod, 0.0)
            tail_cols = tail_cols - mat_prod('rd,dc->rc', v_mat, inner_prod)
            first_blk = jnp.where(is_owner, fac_panel, tail_cols[:, :blk_width])
            work_mat = jnp.concatenate([work_mat[:, :col_lo], first_blk, tail_cols[:, blk_width:]], axis=1)
            tau_parts.append(tau_vec)
        panels_new = work_mat[:, :panel_cols].reshape(n_rows, per_col, blk_width)
        return panels_new, work_mat[:, panel_cols:], jnp.concatenate(tau_parts)

    return jax.shard_map(local_run, mesh=mesh, in_specs=(P('pr', 'pc', None), P('pr', 'pc')), out_specs=(P('pr', 'pc', None), P('pr', 'pc'), P()), check_vma=False)
```

profile of v0, /device:TPU:0, one launch (start us, length us, event | category | flops | bytes accessed | tf_op | source)
XLA Modules:
  0.0 4555.6 jit_solution(4041430764979769711)
XLA Ops:
  8.5 1960.3 %while.64 = (s32[]{:T(128)}, f32[4096,64]{0,1:T(8,128)S(1)}, f32[64]{0:T(128)S(1)}, s32[]{:T(128)}, s32[]{:T(128)}, /*index=5*/f32[]{:T(128)}, s32[]{:T(128)}) while((s32[]{:T(128)}, f32[4096,64]{0,1:T(8,128)S(1)}, f32[64]{0:T(128)S(1)}, s32[]{:T(128)}, s32[]{:T(128)}, /*index=5*/f32[]{:T(128)}, s32[]{:T(128)}) %tuple.161), condition=%wide.region_5.6_spmd.clone.clone, body=%wide.region_0.5_spmd.clone.clone.sunk | while | flops 4022795 | bytes 3344801 | solution.py:38
  10.6 15.4 psum.104
  152.7 11.8 psum.105
  305.6 11.8 psum.105
  580.7 11.8 psum.105
  733.6 11.8 psum.105
  886.5 11.8 psum.105
  1161.6 11.8 psum.105
  1314.5 11.8 psum.105
  1970.0 22.4 psum.86
  1992.4 138.1 %while.65 = (s32[]{:T(128)}, f32[64,64]{1,0:T(8,128)S(1)}, f32[64]{0:T(128)S(1)}, f32[64,64]{0,1:T(8,128)S(1)}, s32[]{:T(128)}, /*index=5*/s32[]{:T(128)}) while((s32[]{:T(128)}, f32[64,64]{1,0:T(8,128)S(1)}, f32[64]{0:T(128)S(1)}, f32[64,64]{0,1:T(8,128)S(1)}, s32[]{:T(128)}, /*index=5*/s32[]{:T(128)}) %tuple.164), condition=%wide.region_9.10_spmd.clone.clone, body=%wide.region_7.9_spmd.clone.clone.sunk | while | flops 62019 | bytes 69615 | solution.py:57
  2134.1 36.0 all-reduce.5.cloned.1.call-done
  2170.1 36.2 fusion.49
  2206.6 46.8 %all-reduce.7.cloned.1.call-done = f32[64,2048]{1,0:T(8,128)} async-done(((f32[64,2048]{1,0:T(8,128)}), f32[64,2048]{1,0:T(8,128)}) %all-reduce.7.cloned.1.call-update) | async-done | bytes 524304 | tf_op jit(solution)/shard_map/psum | solution.py:84
  2255.0 33.8 fusion.48
  2290.3 1913.2 %while.66 = (s32[]{:T(128)}, f32[4096,64]{0,1:T(8,128)S(1)}, f32[64]{0:T(128)S(1)}, s32[]{:T(128)}, s32[]{:T(128)}, /*index=5*/s32[]{:T(128)}, f32[]{:T(128)}, s32[]{:T(128)}) while((s32[]{:T(128)}, f32[4096,64]{0,1:T(8,128)S(1)}, f32[64]{0:T(128)S(1)}, s32[]{:T(128)}, s32[]{:T(128)}, /*index=5*/s32[]{:T(128)}, ...), condition=%wide.region_17.18_spmd.clone.clone, body=%wide.region_12.17_spmd.clone.clone.sunk | while | flops 4022796 | bytes 3344821 | solution.py:38
  4204.8 22.4 psum.89
  4227.2 138.1 %while.67 = (s32[]{:T(128)}, f32[64,64]{1,0:T(8,128)S(1)}, f32[64]{0:T(128)S(1)}, f32[64,64]{0,1:T(8,128)S(1)}, s32[]{:T(128)}, /*index=5*/s32[]{:T(128)}) while((s32[]{:T(128)}, f32[64,64]{1,0:T(8,128)S(1)}, f32[64]{0:T(128)S(1)}, f32[64,64]{0,1:T(8,128)S(1)}, s32[]{:T(128)}, /*index=5*/s32[]{:T(128)}) %tuple.170), condition=%wide.region_21.22_spmd.clone.clone, body=%wide.region_19.21_spmd.clone.clone.sunk | while | flops 62019 | bytes 69615 | solution.py:57
  4367.9 22.7 slice.79
  4390.6 15.5 all-reduce.9.cloned.1.call-done
  4406.1 36.4 fusion.47
  4444.2 45.4 all-reduce.11.cloned.1.call-done
  4491.2 32.9 fusion.46
  4526.4 22.7 slice.83
  (2339 shorter events, 3643.6 us)
Async XLA Ops:
  7.2 2163.0 %all-reduce.5.cloned.1.call-start = ((), (), s32[]{:S(2)}) async-start(), calls=%async_computation | async-start | bytes 2162688 | tf_op jit(solution)/shard_map/psum | solution.py:79
  8.5 2246.6 %copy-start = (f32[4096,1,64]{0,2,1:T(8,128)S(1)}, f32[4096,1,64]{0,2,1:T(8,128)}, u32[]{:S(2)}) copy-start(f32[4096,1,64]{0,2,1:T(8,128)} %param.10) | copy-start | bytes 3145732
  2134.1 119.3 %all-reduce.7.cloned.1.call-start = ((), (), s32[]{:S(2)}) async-start(), calls=%async_computation.1 | async-start | bytes 1048576 | tf_op jit(solution)/shard_map/psum | solution.py:84
  2206.3 2199.8 %all-reduce.9.cloned.1.call-start = ((), (), s32[]{:S(2)}) async-start(), calls=%async_computation.2 | async-start | bytes 2162688 | tf_op jit(solution)/shard_map/psum | solution.py:79
  4367.6 121.9 %all-reduce.11.cloned.1.call-start = ((), (), s32[]{:S(2)}) async-start(), calls=%async_computation.3 | async-start | bytes 1048576 | tf_op jit(solution)/shard_map/psum | solution.py:84
  4406.1 37.3 copy-start.1
Sparse Core Ops, SparseCore 0:
  2134.2 35.8 all-reduce.4
  2206.4 46.9 all-reduce.6
  4367.8 38.2 all-reduce.8
  4442.6 46.9 all-reduce.10
where the time goes:
time: 4570 us; the launch traced here: 4560 us
  blocking collectives  3070 us (67%)
  loops' own time  427 us (9%)
  other arithmetic  410 us (9%)
  matrix products  362 us (8%)
  waiting for transfers between devices  144 us (3%)
  local copies, waits for them, and re-layouts  133 us (3%)
    psum x128, blocking collectives, column_step(): sum_stats = lax.psum(local_stats, 'pr')  1510 us
    psum x128, blocking collectives, column_step(): proj_row = lax.psum(mat_prod('r,rc->c', house_vec, fac_panel), 'pr')  1510 us
    dot_general x264, matrix products, mat_prod(): jnp.einsum(form, left, right, precision=FULL_PRECISION, preferred_element...  362 us
    another operation x2, loops' own time, factor_panel(): lax.fori_loop(0, blk_width, column_step, (panel_blk, jnp.zeros((blk_width...  342 us
    another operation x128, other arithmetic, column_step(): jnp.stack([jnp.sum(jnp.where(row_ids >= diag_row, column * column, 0.0)),...  172 us
    psum x2, waiting for transfers between devices, local_run(): inner_prod = lax.psum(mat_prod('rb,rc->bc', v_mat, tail_cols), 'pr')  92.2 us
  transfers between devices with their start and end apart: 4, of which 4 were waited for; matrix products, arithmetic and copies ran while one was open for 1% of the time, Pallas kernels for 0%

commit v1 on v0

v1 whole, which is shorter than its diff:
```python
import jax
import jax.numpy as jnp
from jax import lax
from jax.experimental import pallas as pl
from jax.experimental.pallas import tpu as pltpu
from jax.sharding import PartitionSpec as P

FULL_PRECISION = lax.Precision.HIGHEST
MESH = pl.DeviceIdType.MESH
ROWS, NB, NP, TRAIL = 4096, 64, 128, 1984
NPR = 8
LANES = 1024
NCH = ROWS // LANES
OWN = TRAIL // NPR
MROWS = 496
MSG = NP + 8


def mat_prod(form, left, right):
    return jnp.einsum(form, left, right, precision=FULL_PRECISION, preferred_element_type=jnp.float32)


def fdot(a, b):
    return jnp.dot(a, b, precision=FULL_PRECISION, preferred_element_type=jnp.float32)


def bdot(a, b):
    return jnp.dot(a, b, preferred_element_type=jnp.float32)


def split3(x):
    hi = x.astype(jnp.bfloat16)
    rest = x - hi.astype(jnp.float32)
    mid = rest.astype(jnp.bfloat16)
    low = (rest - mid.astype(jnp.float32)).astype(jnp.bfloat16)
    return hi, mid, low


def dot_parts(x, pieces):
    hi, mid, low = split3(x)
    d1 = bdot(hi, pieces)
    d2 = bdot(mid, pieces[:, :2 * NP])
    d3 = bdot(low, pieces[:, :NP])
    return d1[:, :NP] + ((d1[:, NP:2 * NP] + d2[:, :NP]) + ((d1[:, 2 * NP:] + d3) + d2[:, NP:]))


def unit_tri_inv(strict, eye):
    inv = eye + strict
    power = strict
    for _ in range(6):
        power = fdot(power, power)
        inv = inv + fdot(inv, power)
    return inv


def eye_of(n):
    return lax.broadcasted_iota(jnp.int32, (n, n), 0) == lax.broadcasted_iota(jnp.int32, (n, n), 1)


def factor_steps(h_s, b_s, r_s, u_s, row0, start, stop):
    n_rows = NP - row0
    lane1 = lax.broadcasted_iota(jnp.int32, (1, NP), 1)
    lane = lax.broadcasted_iota(jnp.int32, (n_rows, NP), 1)

    def step(j, carry):
        idx = jnp.full((n_rows, NP), j, jnp.int32)
        idx8 = jnp.full((8, NP), j, jnp.int32)
        hrow = h_s[pl.ds(j, 1), :]
        brow = b_s[pl.ds(j, 1), :]
        hjj = jnp.take_along_axis(jnp.broadcast_to(hrow, (8, NP)), idx8, axis=1)[:1]
        alpha = jnp.take_along_axis(jnp.broadcast_to(brow, (8, NP)), idx8, axis=1)[:1]
        hcol = jnp.take_along_axis(h_s[row0:, :], idx, axis=1)
        bcol = jnp.take_along_axis(b_s[row0:, :], idx, axis=1)
        root = lax.rsqrt(hjj)
        root = root * (1.5 - 0.5 * hjj * root * root)
        beta = jnp.where(alpha >= 0.0, -hjj * root, hjj * root)
        invb = jnp.where(alpha >= 0.0, -root, root)
        invd = 1.0 / (alpha - beta)
        keep = lane1 >= j
        rrow = jnp.where(keep, hrow * invb, 0.0)
        urow = jnp.where(keep, brow - rrow, 0.0)
        r_s[pl.ds(j, 1), :] = rrow
        u_s[pl.ds(j, 1), :] = urow
        h_s[row0:, :] = h_s[row0:, :] - hcol * (rrow * invb)
        vcol = bcol * invd
        b_s[row0:, :] = jnp.where(lane == j, vcol, b_s[row0:, :] - vcol * urow)
        return carry

    lax.fori_loop(start, stop, step, 0)


def reduce_kernel(panel_hbm, trail_hbm, pt_out, wt_out, zt_out, tops_out, tau_out, bad_out,
                  cbuf, pt, pp, gown, gin, gsum, ptop, ct, part, rin, part2, rsum, st, h_s, b_s, r_s, u_s, cmx,
                  csem, psem, zsend, zrecv, osem, gsend, grecv, tsend, trecv, csend, crecv, r1sem, r2send, r2recv,
                  casend, carecv, sasend, sarecv, msem):
    me = lax.axis_index('pr')
    q = lax.axis_index('pc')
    core = lax.rem(me, 2)
    chip = (me - core) // 2
    twin = me + 1 - 2 * core
    partner = {'pc': 1 - q}
    mine = pl.ds(pl.multiple_of(q * NB, NB), NB)
    theirs = pl.ds(pl.multiple_of((1 - q) * NB, NB), NB)

    def remote(src, dst, s_sem, r_sem, dev):
        return pltpu.make_async_remote_copy(src_ref=src, dst_ref=dst, send_sem=s_sem, recv_sem=r_sem, device_id=dev, device_id_type=MESH)

    def lanes(c):
        return pl.ds(c * LANES, LANES)

    def load_trail(c):
        return pltpu.make_async_copy(trail_hbm.at[:, lanes(c)], cbuf.at[:, lanes(c)], csem.at[c])

    def load_panel(c):
        return pltpu.make_async_copy(panel_hbm.at[:, lanes(c)], pt.at[mine, lanes(c)], psem.at[c])

    def send_panel(c):
        return remote(pt.at[mine, lanes(c)], pt.at[mine, lanes(c)], zsend.at[c], zrecv.at[c], partner)

    def recv_panel(c):
        return remote(pt.at[theirs, lanes(c)], pt.at[theirs, lanes(c)], zsend.at[c], zrecv.at[c], partner)

    for c in range(NCH):
        load_panel(c).start()
    for c in range(NCH):
        load_trail(c).start()

    barrier = pltpu.get_barrier_semaphore()
    pl.semaphore_signal(barrier, inc=1, device_id=partner, device_id_type=MESH)
    for d in range(1, NPR):
        pl.semaphore_signal(barrier, inc=1, device_id={'pr': lax.rem(me + d, NPR)}, device_id_type=MESH)
    pl.semaphore_wait(barrier, NPR)
    for c in range(NCH):
        load_panel(c).wait()
        send_panel(c).start()

    def gather_start(buf, ssem, rsem):
        for d in range(4):
            dev = twin if d == 0 else lax.rem(me + 2 * d, NPR)
            remote(buf.at[me], buf.at[me], ssem.at[d], rsem.at[me], {'pr': dev}).start()

    def gather_forward(buf, ssem, rsem):
        for d in range(1, 4):
            src = lax.rem(me + NPR - 2 * d, NPR)
            remote(buf.at[src], buf.at[src], ssem.at[3 + d], rsem.at[src], {'pr': twin}).wait_recv()
            remote(buf.at[src], buf.at[src], ssem.at[3 + d], rsem.at[src], {'pr': twin}).start()

    def gather_wait(buf, ssem, rsem):
        for d in range(4):
            src = lax.rem(twin + NPR - 2 * d, NPR)
            remote(buf.at[src], buf.at[src], ssem.at[d], rsem.at[src], {'pr': twin}).wait_recv()

    def gather_end(buf, ssem, rsem):
        for d in range(7):
            remote(buf.at[me], buf.at[me], ssem.at[d], rsem.at[me], {'pr': twin}).wait_send()

    def share_top(i):
        return remote(pt.at[:, pl.ds(0, NP)], ptop, tsend.at[i], trecv, {'pr': i})

    def scatter_top(i):
        return remote(cbuf.at[pl.ds(i * OWN, OWN), pl.ds(0, NP)], ct.at[i], csend.at[i], crecv, {'pr': i})

    part[...] = jnp.zeros_like(part)
    gown[...] = jnp.zeros_like(gown)

    def make_pieces(c):
        hi, mid, low = split3(pt[:, lanes(c)].T)
        pp[:, :NP] = hi
        pp[:, NP:2 * NP] = mid
        pp[:, 2 * NP:] = low
        gown[:NP, :] += dot_parts(pt[:, lanes(c)], pp[...])

    def product(c, first, last):
        def rows_step(m, carry):
            rows = pl.ds(pl.multiple_of(m * MROWS, MROWS), MROWS)
            got = dot_parts(cbuf[rows, lanes(c)], pp[...])
            part[m] += got.reshape(2, OWN, NP)
            return carry

        lax.fori_loop(first, last, rows_step, 0)

    cmax = jnp.zeros((8, LANES), jnp.float32)
    for c in range(NCH):
        load_trail(c).wait()
        if c == 0:
            @pl.when(me == 0)
            def _():
                ct[0] = cbuf[:OWN, :NP]
                for i in range(1, NPR):
                    scatter_top(i).start()

        def largest(m, acc):
            x = cbuf[pl.ds(pl.multiple_of(m * OWN, OWN), OWN), lanes(c)]
            return jnp.maximum(acc, jnp.max(jnp.abs(x).reshape(OWN // 8, 8, LANES), axis=0))

        cmax = lax.fori_loop(0, NPR, largest, cmax)
        if c == 1:
            @pl.when(me != 0)
            def _():
                remote(ct.at[me], ct.at[me], csend.at[0], crecv, {'pr': 0}).wait_recv()

            gather_start(ct, casend, carecv)
        if c == 3:
            gather_forward(ct, casend, carecv)
        recv_panel(c).wait_recv()
        if c == 0:
            @pl.when(me == 0)
            def _():
                ptop[...] = pt[:, :NP]
                for i in range(1, NPR):
                    share_top(i).start()
        make_pieces(c)
        if c < NCH - 1:
            product(c, 0, 4)

    big = jnp.max(jnp.max(cmax, axis=1, keepdims=True), axis=0, keepdims=True)
    gown[NP:, :] = jnp.broadcast_to(big, (8, NP))

    gcopy = remote(gown, gin, gsend.at[0], grecv.at[4], {'pr': twin})
    gcopy.start()
    pt_copy = pltpu.make_async_copy(pt, pt_out, osem)
    pt_copy.start()
    product(NCH - 1, 0, 2)
    gcopy.wait()
    gsum[chip, :NP, :] = gown[:NP, :] + gin[:NP, :]
    gsum[chip, NP:, :] = jnp.maximum(gown[NP:, :], gin[NP:, :])

    def send_gram(d):
        return remote(gsum.at[chip], gsum.at[chip], gsend.at[d], grecv.at[chip], {'pr': lax.rem(me + 2 * d, NPR)})

    for d in range(1, 4):
        send_gram(d).start()
    product(NCH - 1, 2, 4)

    scopy = remote(part.at[:, 1 - core], rin, r1sem.at[0], r1sem.at[1], {'pr': twin})
    scopy.start()

    @pl.when(me != 0)
    def _():
        remote(ptop, ptop, tsend.at[0], trecv, {'pr': 0}).wait_recv()

    for d in range(1, 4):
        src = lax.rem(chip + 4 - d, 4)
        remote(gsum.at[src], gsum.at[src], gsend.at[d], grecv.at[src], {'pr': twin}).wait_recv()
    gram = ((gsum[0, :NP, :] + gsum[1, :NP, :]) + gsum[2, :NP, :]) + gsum[3, :NP, :]
    cmx[0] = jnp.maximum(jnp.maximum(gsum[0, NP:, :], gsum[1, NP:, :]), jnp.maximum(gsum[2, NP:, :], gsum[3, NP:, :]))
    mcopy = remote(cmx.at[0], cmx.at[1], msem.at[0], msem.at[1], partner)
    mcopy.start()

    eyeb = eye_of(NP)
    eye = jnp.where(eyeb, 1.0, 0.0)
    row_id = lax.broadcasted_iota(jnp.int32, (NP, NP), 0)
    col_id = lax.broadcasted_iota(jnp.int32, (NP, NP), 1)

    def newton_rsqrt(x):
        y = lax.rsqrt(x)
        return y * (1.5 - 0.5 * x * y * y)

    gdiag = jnp.where(eyeb, gram, 0.0)
    g_row = jnp.sum(gdiag, axis=0, keepdims=True)
    g_col = jnp.sum(gdiag, axis=1, keepdims=True)
    n_row, n_col = newton_rsqrt(g_row), newton_rsqrt(g_col)
    h_s[...] = (gram * n_row) * n_col
    b_s[...] = ptop[...].T * n_row
    factor_steps(h_s, b_s, r_s, u_s, 0, 0, 16)

    scopy.wait()
    for s in range(4):
        part2[s] = part[s, core] + rin[s]

    def scatter_part(d):
        to = lax.rem(chip + d, 4)
        return remote(part2.at[to], rsum.at[chip], r2send.at[d], r2recv.at[chip], {'pr': 2 * to + core})

    for d in range(1, 4):
        scatter_part(d).start()
    factor_steps(h_s, b_s, r_s, u_s, 0, 16, 64)
    rsum[chip] = part2[chip]
    for d in range(1, 4):
        src = lax.rem(chip + 4 - d, 4)
        remote(part2.at[src], rsum.at[src], r2send.at[d], r2recv.at[src], {'pr': twin}).wait_recv()
    st[me] = ((rsum[0] + rsum[1]) + rsum[2]) + rsum[3]
    gather_start(st, sasend, sarecv)
    factor_steps(h_s, b_s, r_s, u_s, NB, 64, 120)
    gather_forward(st, sasend, sarecv)
    gather_wait(ct, casend, carecv)
    factor_steps(h_s, b_s, r_s, u_s, NB, 120, 128)

    rmat, umat = r_s[...], u_s[...]
    lstrict = jnp.where(row_id > col_id, b_s[...], 0.0)
    lmat = eye + lstrict

    def upper_inv(mat):
        diag = jnp.where(eyeb, mat, 0.0)
        d_row = 1.0 / jnp.sum(diag, axis=0, keepdims=True)
        d_col = 1.0 / jnp.sum(diag, axis=1, keepdims=True)
        return unit_tri_inv(jnp.where(col_id > row_id, -(mat * d_col), 0.0), eye) * d_row

    rinv = upper_inv(rmat)
    uinv = upper_inv(umat)
    linv = unit_tri_inv(-lstrict, eye)
    wt_out[...] = (uinv * n_col).T
    linv_t = linv.T
    m2_t = (fdot(linv, rinv.T) * n_row).T
    tau_out[...] = jnp.sum(jnp.where(eyeb, -umat / rmat, 0.0), axis=0, keepdims=True)
    tops_out[:NP, :] = lmat.T
    tops_out[NP:, :] = jnp.where(row_id > col_id, lmat, rmat * (g_row * n_row)).T

    mcopy.wait()
    c_top = jnp.max(jnp.maximum(cmx[0], cmx[1]), axis=1, keepdims=True)[:1]
    g_max = jnp.max(g_row, axis=1, keepdims=True)
    g_min = jnp.min(g_row, axis=1, keepdims=True)

    def total_of(x):
        return jnp.sum(jnp.sum(x, axis=1, keepdims=True), axis=0, keepdims=True)

    resid = total_of(jnp.abs(fdot(rinv, rmat) - eye) + jnp.abs(fdot(uinv, umat) - eye) + jnp.abs(fdot(linv, lmat) - eye))
    cond = total_of(rinv * rinv + uinv * uinv + linv * linv)
    good = (g_max < 1e12) & (g_min > 1e-12) & (resid < 1e-3) & (cond < 2048.0)
    good = good & (c_top < 1e26) & ((c_top > 1e-20) | (c_top == 0.0))
    bad_out[...] = jnp.broadcast_to(jnp.where(good, 0.0, 1.0), (8, NP))

    gather_wait(st, sasend, sarecv)

    def make_z(i, carry):
        zt_out[pl.ds(pl.multiple_of(i * OWN, OWN), OWN), :] = fdot(ct[i], linv_t) - fdot(st[i], m2_t)
        return carry

    lax.fori_loop(0, NPR, make_z, 0)

    pt_copy.wait()
    for c in range(NCH):
        send_panel(c).wait_send()
    gather_end(ct, casend, carecv)
    gather_end(st, sasend, sarecv)
    for d in range(1, 4):
        send_gram(d).wait_send()
        scatter_part(d).wait_send()

    @pl.when(me == 0)
    def _():
        for i in range(1, NPR):
            share_top(i).wait_send()
            scatter_top(i).wait_send()


def reduce_call(panel_t, trail_t):
    f32 = jnp.float32
    dma = pltpu.SemaphoreType.DMA
    vmem = pl.BlockSpec(memory_space=pltpu.VMEM)
    hbm = pl.BlockSpec(memory_space=pl.ANY)
    return pl.pallas_call(
        reduce_kernel,
        out_shape=(
            jax.ShapeDtypeStruct((NP, ROWS), f32), jax.ShapeDtypeStruct((NP, NP), f32), jax.ShapeDtypeStruct((TRAIL, NP), f32),
            jax.ShapeDtypeStruct((2 * NP, NP), f32), jax.ShapeDtypeStruct((1, NP), f32), jax.ShapeDtypeStruct((8, NP), f32)),
        in_specs=[hbm, hbm],
        out_specs=(hbm, vmem, vmem, vmem, vmem, vmem),
        scratch_shapes=[
            pltpu.VMEM((TRAIL, ROWS), f32), pltpu.VMEM((NP, ROWS), f32), pltpu.VMEM((LANES, 3 * NP), jnp.bfloat16),
            pltpu.VMEM((MSG, NP), f32), pltpu.VMEM((MSG, NP), f32), pltpu.VMEM((4, MSG, NP), f32), pltpu.VMEM((NP, NP), f32),
            pltpu.VMEM((NPR, OWN, NP), f32), pltpu.VMEM((4, 2, OWN, NP), f32), pltpu.VMEM((4, OWN, NP), f32), pltpu.VMEM((4, OWN, NP), f32),
            pltpu.VMEM((4, OWN, NP), f32), pltpu.VMEM((NPR, OWN, NP), f32),
            pltpu.VMEM((NP, NP), f32), pltpu.VMEM((NP, NP), f32), pltpu.VMEM((NP, NP), f32), pltpu.VMEM((NP, NP), f32), pltpu.VMEM((2, 8, NP), f32),
            dma((NCH,)), dma((NCH,)), dma((NCH,)), dma((NCH,)), dma(()), dma((4,)), dma((5,)), dma((NPR,)), dma(()), dma((NPR,)), dma(()),
            dma((2,)), dma((4,)), dma((4,)), dma((7,)), dma((NPR,)), dma((7,)), dma((NPR,)), dma((2,))],
        compiler_params=pltpu.CompilerParams(collective_id=0, has_side_effects=True, vmem_limit_bytes=67043328),
        name='reduce',
    )(panel_t, trail_t)


UL = 512


def update_kernel(pt_ref, wt_ref, zt_ref, tops_ref, c_ref, o_ref, pan_ref, zcat, vcat):
    first = pl.program_id(0) == 0
    q = lax.axis_index('pc')

    @pl.when(first)
    def _():
        zh, zm, zl = split3(zt_ref[...])
        for n, piece in enumerate((zh, zh, zm, zm, zl, zh)):
            zcat[:, n * NP:(n + 1) * NP] = piece

    v = fdot(wt_ref[...], pt_ref[...])
    at_top = first & (lax.axis_index('pr') == 0)
    lane = lax.broadcasted_iota(jnp.int32, (NP, UL), 1)
    inside = (lane < NP) & at_top
    pad = jnp.zeros((NP, UL - NP), jnp.float32)
    stored = jnp.where(inside, jnp.concatenate([tops_ref[NP:, :], pad], axis=1), v)
    v = jnp.where(inside, jnp.concatenate([tops_ref[:NP, :], pad], axis=1), v)
    pan_ref[...] = jnp.where(q == 0, stored[:NB], stored[NB:])
    vh, vm, vl = split3(v)
    for n, piece in enumerate((vh, vm, vh, vm, vh, vl)):
        vcat[n * NP:(n + 1) * NP, :] = piece

    def rows_step(m, carry):
        rows = pl.ds(pl.multiple_of(m * MROWS, MROWS), MROWS)
        o_ref[rows, :] = c_ref[rows, :] - bdot(zcat[rows, :], vcat[...])
        return carry

    lax.fori_loop(0, TRAIL // MROWS, rows_step, 0)


def update_call(pt, wt, zt, tops, trail_t):
    f32 = jnp.float32
    return pl.pallas_call(
        update_kernel,
        out_shape=(jax.ShapeDtypeStruct((TRAIL, ROWS), f32), jax.ShapeDtypeStruct((NB, ROWS), f32)),
        grid=(ROWS // UL,),
        in_specs=[pl.BlockSpec((NP, UL), lambda i: (0, i)), pl.BlockSpec((NP, NP), lambda i: (0, 0)), pl.BlockSpec((TRAIL, NP), lambda i: (0, 0)),
                  pl.BlockSpec((2 * NP, NP), lambda i: (0, 0)), pl.BlockSpec((TRAIL, UL), lambda i: (0, i))],
        out_specs=(pl.BlockSpec((TRAIL, UL), lambda i: (0, i)), pl.BlockSpec((NB, UL), lambda i: (0, i))),
        scratch_shapes=[pltpu.VMEM((TRAIL, 6 * NP), jnp.bfloat16), pltpu.VMEM((6 * NP, UL), jnp.bfloat16)],
        compiler_params=pltpu.CompilerParams(dimension_semantics=('arbitrary',), vmem_limit_bytes=40 << 20),
        name='update',
    )(pt, wt, zt, tops, trail_t)


def sum_rows(x):
    for bit in (1, 2, 4):
        x = x + lax.ppermute(x, 'pr', [(i, i ^ bit) for i in range(NPR)])
    return x


def from_owner(x, owner):
    x = jnp.where(lax.axis_index('pc') == owner, x, 0.0)
    return x + lax.ppermute(x, 'pc', [(0, 1), (1, 0)])


def factor_panel(panel_blk, row_ids, first_row):
    col_ids = jnp.arange(NB)

    def column_step(j, carry):
        fac_panel, tau_vec = carry
        diag_row = first_row + j
        column = lax.dynamic_slice_in_dim(fac_panel, j, 1, axis=1)[:, 0]
        below_diag = row_ids > diag_row
        at_diag = row_ids == diag_row
        stats = sum_rows(jnp.stack([jnp.sum(jnp.where(row_ids >= diag_row, column * column, 0.0)), jnp.sum(jnp.where(at_diag, column, 0.0))]))
        diag_val = stats[1]
        col_norm = jnp.sqrt(stats[0])
        beta_val = jnp.where(diag_val >= 0.0, -col_norm, col_norm)
        tau_j = (beta_val - diag_val) / beta_val
        house_vec = jnp.where(below_diag, column / (diag_val - beta_val), jnp.where(at_diag, 1.0, 0.0))
        proj_row = sum_rows(jnp.sum(house_vec[:, None] * fac_panel, axis=0))
        proj_row = jnp.where(col_ids > j, tau_j * proj_row, 0.0)
        fac_panel = fac_panel - house_vec[:, None] * proj_row[None, :]
        new_col = jnp.where(below_diag, house_vec, jnp.where(at_diag, beta_val, column))
        fac_panel = jnp.where(col_ids[None, :] == j, new_col[:, None], fac_panel)
        return fac_panel, jnp.where(col_ids == j, tau_j, tau_vec)

    return lax.fori_loop(0, NB, column_step, (panel_blk, jnp.zeros((NB,), jnp.float32)))


def build_t(gram_mat, tau_vec):
    col_ids = jnp.arange(NB)

    def t_step(j, t_mat):
        g_col = jnp.where(col_ids < j, lax.dynamic_slice_in_dim(gram_mat, j, 1, axis=1)[:, 0], 0.0)
        tau_j = jnp.sum(jnp.where(col_ids == j, tau_vec, 0.0))
        new_col = jnp.where(col_ids == j, tau_j, -tau_j * jnp.sum(t_mat * g_col[None, :], axis=1))
        return jnp.where(col_ids[None, :] == j, new_col[:, None], t_mat)

    return lax.fori_loop(0, NB, t_step, jnp.zeros((NB, NB), jnp.float32))


def by_columns(panel, trail):
    col_idx = lax.axis_index('pc')
    row_ids = lax.axis_index('pr') * ROWS + jnp.arange(ROWS)
    v_parts, z_parts, taus = [], [], []
    for k in range(2):
        fac_panel, tau_vec = factor_panel(panel, row_ids, k * NB)
        diag = k * NB + jnp.arange(NB)
        v_mat = jnp.where(row_ids[:, None] > diag[None, :], fac_panel, jnp.where(row_ids[:, None] == diag[None, :], 1.0, 0.0))
        v_mat = from_owner(v_mat, k)
        tau_vec = from_owner(tau_vec, k)
        t_mat = build_t(sum_rows(mat_prod('rb,rc->bc', v_mat, v_mat)), tau_vec)
        inner = mat_prod('bd,bc->dc', t_mat, sum_rows(mat_prod('rb,rc->bc', v_mat, trail)))
        if k == 0:
            trail = trail - mat_prod('rd,dc->rc', v_mat, inner)
            near = mat_prod('bd,bc->dc', t_mat, sum_rows(mat_prod('rb,rc->bc', v_mat, panel)))
            later = panel - mat_prod('rd,dc->rc', v_mat, near)
            panel = jnp.where(col_idx == 0, fac_panel, later)
        else:
            panel = jnp.where(col_idx == 1, fac_panel, panel)
        v_parts.append(v_mat)
        z_parts.append(inner)
        taus.append(tau_vec)
    v_t = jnp.concatenate(v_parts, axis=1).T
    top = panel[:NP].T
    tops = jnp.concatenate([v_t[:, :NP], top, top], axis=0)
    return v_t, jnp.eye(NP, dtype=jnp.float32), jnp.concatenate(z_parts, axis=0).T, tops, jnp.concatenate(taus)[None, :]


def solution(mesh):
    def local_run(panels_loc, trail_loc):
        panel_t = panels_loc.reshape(ROWS, NB).T
        trail_t = trail_loc.T
        pt, wt, zt, tops, tau, bad = reduce_call(panel_t, trail_t)

        def direct(pt, wt, zt, tops, tau, trail_t, panel_t):
            return update_call(pt, wt, zt, tops, trail_t) + (tau,)

        def again(pt, wt, zt, tops, tau, trail_t, panel_t):
            pt, wt, zt, tops, tau = by_columns(panel_t.T, trail_t.T)
            return update_call(pt, wt, zt, tops, trail_t) + (tau,)

        trail_new, pan, tau = lax.cond(bad[0, 0] > 0.0, again, direct, pt, wt, zt, tops, tau, trail_t, panel_t)
        return pan.T.reshape(ROWS, 1, NB), trail_new.T, tau.reshape(NP)

    return jax.shard_map(local_run, mesh=mesh, in_specs=(P('pr', 'pc', None), P('pr', 'pc')), out_specs=(P('pr', 'pc', None), P('pr', 'pc'), P()), check_vma=False)
```

time: 4570 us -> 100 us (0.02)
  blocking collectives: 3070 us -> 0 us
  loops' own time: 427 us -> 0.19 us
  other arithmetic: 410 us -> 0 us
  matrix products: 362 us -> 0 us
  waiting for transfers between devices: 144 us -> 0 us
  local copies, waits for them, and re-layouts: 133 us -> 2.33 us
  Pallas kernels: 0 us -> 95.9 us
    psum x258 -> x0, blocking collectives: 3070 us -> none  [the longest x128 1510 us: column_step(): sum_stats = lax.psum(local_stats, 'pr')]
    another operation x4 -> x1, loops' own time: 427 us -> 0.19 us  [local_run(): lax.cond(bad[0, 0] > 0.0, again, direct, pt, wt, zt, tops, tau, trail_t,...]
    dot_general x264 -> x0, matrix products: 362 us -> none  [mat_prod(): jnp.einsum(form, left, right, precision=FULL_PRECISION, preferred_element...]
    another operation x128 -> x0, other arithmetic: 172 us -> none  [column_step(): jnp.stack([jnp.sum(jnp.where(row_ids >= diag_row, column * column, 0.0)),...]
    reduce_sum x256 -> x0, other arithmetic: 161 us -> none  [the longest x128 83.1 us: column_step(): jnp.sum(jnp.where(row_ids >= diag_row, column * column, 0.0))]
    psum x4 -> x0, waiting for transfers between devices: 144 us -> none  [the longest x2 92.2 us: local_run(): inner_prod = lax.psum(mat_prod('rb,rc->bc', v_mat, tail_cols), 'pr')]
    slice x132 -> x1, local copies, waits for them, and re-layouts: 126 us -> 1.19 us  [local_run(): bad[0, 0] > 0.0]
    pallas_call x0 -> x2, Pallas kernels: none -> 95.9 us  [the longest x1 65.4 us: reduce_call(): pl.pallas_call(reduce_kernel, out_shape=(jax.ShapeDtypeStruct((NP, ROWS),...]
  transfers between devices with their start and end apart: 4 -> 0, of which waited for: 4 -> 0; matrix products, arithmetic and copies ran while one was open for 1% -> 0% of each run, Pallas kernels for 0% -> 0%
where the time goes in v1:
time: 100 us; the launch traced here: 99.8 us
  Pallas kernels  95.9 us (96%)
  local copies, waits for them, and re-layouts  2.33 us (2%)
  between operations  1.29 us (1%)
    pallas_call x1, Pallas kernels, reduce_call(): pl.pallas_call(reduce_kernel, out_shape=(jax.ShapeDtypeStruct((NP, ROWS),...  65.4 us
    pallas_call x1, Pallas kernels, update_call(): pl.pallas_call(update_kernel, out_shape=(jax.ShapeDtypeStruct((TRAIL, ROW...  30.6 us

profile of v1, /device:TPU:0, one launch (start us, length us, event | category | flops | bytes accessed | tf_op | source)
XLA Modules:
  0.0 99.8 jit_solution(13711261740611110920)
XLA Ops:
  0.6 65.4 %reduce.1 = (f32[128,4096]{1,0:T(8,128)}, f32[128,128]{1,0:T(8,128)}, f32[1984,128]{1,0:T(8,128)}, f32[256,128]{1,0:T(8,128)}, f32[1,128]{1,0:T(1,128)}, /*index=5*/f32[8,128]{1,0:T(8,128)}) custom-call(f32[64,4096]{1,0:T(8,128)} %bitcast.89, f32[1984,4096]{1,0:T(8,128)} %bitcast.84), custom_call_target="tpu_custom_call" | custom-call | tf_op jit(solution)/shard_map/reduce/pallas_call | solution.py:352
  66.0 1.2 %slice.37 = f32[1,1]{1,0:T(1,128)} slice(f32[8,128]{1,0:T(8,128)} %get-tuple-element.433), slice={[0:1], [0:1]} | slice | bytes 8 | tf_op jit(solution)/shard_map/slice | solution.py:509
  67.9 30.8 %conditional.1 = (f32[1984,4096]{1,0:T(8,128)}, f32[64,4096]{1,0:T(8,128)}, f32[1,128]{1,0:T(1,128)}) conditional(s32[]{:T(128)} %bitcast.7, (f32[128,4096]{1,0:T(8,128)}, f32[128,128]{1,0:T(8,128)}, f32[1984,128]{1,0:T(8,128)}, f32[256,128]{1,0:T(8,128)}, f32[1984,4096]{1,0:T(8,128)}, /*index=5*/f32[1,128]{1,0:T(1,128)}) %tuple.189, ...), branch_computations={%region_0.0_spmd, %region_1.20_spmd} | conditional | flops 19745761280 | bytes 291303488 | solution.py:509
  68.1 30.6 %update.2 = (f32[1984,4096]{1,0:T(8,128)}, f32[64,4096]{1,0:T(8,128)}) custom-call(f32[128,4096]{1,0:T(8,128)} %get-tuple-element.374.pt_ref, f32[128,128]{1,0:T(8,128)} %get-tuple-element.375.wt_ref, f32[1984,128]{1,0:T(8,128)} %get-tuple-element.376.zt_ref, f32[256,128]{1,0:T(8,128)} %get-tuple-element.377.tops_ref, f32[1984,4096]{1,0:T(8,128)} %get-tuple-element.378.c_ref), custom_call_target="tpu_custom_call" | custom-call | tf_op jit(solution)/shard_map/cond/branch_0_fun/update/pallas_call | solution.py:407
  98.6 1.1 %copy.60 = f32[128]{0:T(128)} copy(f32[128]{0:T(128)} %bitcast.100) | data formatting | bytes 1024

commit v2 on v1

--- a/solution.py
+++ b/solution.py
@@ -11,6 +11,8 @@
 NPR = 8
 LANES = 1024
 NCH = ROWS // LANES
+AUX0, ALL = TRAIL, TRAIL + NP
+WT0, TOP0, TOP1, TAU0, BAD0 = (16 * NP, 17 * NP, 18 * NP, 19 * NP, 20 * NP)
 OWN = TRAIL // NPR
 MROWS = 496
 MSG = NP + 8
@@ -89,10 +91,11 @@
     lax.fori_loop(start, stop, step, 0)
 
 
-def reduce_kernel(panel_hbm, trail_hbm, pt_out, wt_out, zt_out, tops_out, tau_out, bad_out,
-                  cbuf, pt, pp, gown, gin, gsum, ptop, ct, part, rin, part2, rsum, st, h_s, b_s, r_s, u_s, cmx,
+def reduce_kernel(panel_hbm, trail_hbm, out, pt_out,
+                  pt, pp, gown, gin, gsum, ptop, ct, part, rin, part2, rsum, st, zpart, h_s, b_s, r_s, u_s, cmx,
                   csem, psem, zsend, zrecv, osem, gsend, grecv, tsend, trecv, csend, crecv, r1sem, r2send, r2recv,
                   casend, carecv, sasend, sarecv, msem):
+    cbuf = out.at[pl.ds(0, TRAIL), :]
     me = lax.axis_index('pr')
     q = lax.axis_index('pc')
     core = lax.rem(me, 2)
@@ -134,31 +137,34 @@
         load_panel(c).wait()
         send_panel(c).start()
 
+    def piece(buf, i):
+        return buf.at[pl.ds(pl.multiple_of(i * OWN, 8), OWN), :]
+
     def gather_start(buf, ssem, rsem):
         for d in range(4):
             dev = twin if d == 0 else lax.rem(me + 2 * d, NPR)
-            remote(buf.at[me], buf.at[me], ssem.at[d], rsem.at[me], {'pr': dev}).start()
+            remote(piece(buf, me), piece(buf, me), ssem.at[d], rsem.at[me], {'pr': dev}).start()
 
     def gather_forward(buf, ssem, rsem):
         for d in range(1, 4):
             src = lax.rem(me + NPR - 2 * d, NPR)
-            remote(buf.at[src], buf.at[src], ssem.at[3 + d], rsem.at[src], {'pr': twin}).wait_recv()
-            remote(buf.at[src], buf.at[src], ssem.at[3 + d], rsem.at[src], {'pr': twin}).start()
+            remote(piece(buf, src), piece(buf, src), ssem.at[3 + d], rsem.at[src], {'pr': twin}).wait_recv()
+            remote(piece(buf, src), piece(buf, src), ssem.at[3 + d], rsem.at[src], {'pr': twin}).start()
 
     def gather_wait(buf, ssem, rsem):
         for d in range(4):
             src = lax.rem(twin + NPR - 2 * d, NPR)
-            remote(buf.at[src], buf.at[src], ssem.at[d], rsem.at[src], {'pr': twin}).wait_recv()
+            remote(piece(buf, src), piece(buf, src), ssem.at[d], rsem.at[src], {'pr': twin}).wait_recv()
 
     def gather_end(buf, ssem, rsem):
         for d in range(7):
-            remote(buf.at[me], buf.at[me], ssem.at[d], rsem.at[me], {'pr': twin}).wait_send()
+            remote(piece(buf, me), piece(buf, me), ssem.at[d], rsem.at[me], {'pr': twin}).wait_send()
 
     def share_top(i):
         return remote(pt.at[:, pl.ds(0, NP)], ptop, tsend.at[i], trecv, {'pr': i})
 
     def scatter_top(i):
-        return remote(cbuf.at[pl.ds(i * OWN, OWN), pl.ds(0, NP)], ct.at[i], csend.at[i], crecv, {'pr': i})
+        return remote(cbuf.at[pl.ds(i * OWN, OWN), pl.ds(0, NP)], piece(ct, i), csend.at[i], crecv, {'pr': i})
 
     part[...] = jnp.zeros_like(part)
     gown[...] = jnp.zeros_like(gown)
@@ -185,7 +191,7 @@
         if c == 0:
             @pl.when(me == 0)
             def _():
-                ct[0] = cbuf[:OWN, :NP]
+                ct[:OWN, :] = cbuf[:OWN, :NP]
                 for i in range(1, NPR):
                     scatter_top(i).start()
 
@@ -197,7 +203,7 @@
         if c == 1:
             @pl.when(me != 0)
             def _():
-                remote(ct.at[me], ct.at[me], csend.at[0], crecv, {'pr': 0}).wait_recv()
+                remote(piece(ct, me), piece(ct, me), csend.at[0], crecv, {'pr': 0}).wait_recv()
 
             gather_start(ct, casend, carecv)
         if c == 3:
@@ -218,8 +224,6 @@
 
     gcopy = remote(gown, gin, gsend.at[0], grecv.at[4], {'pr': twin})
     gcopy.start()
-    pt_copy = pltpu.make_async_copy(pt, pt_out, osem)
-    pt_copy.start()
     product(NCH - 1, 0, 2)
     gcopy.wait()
     gsum[chip, :NP, :] = gown[:NP, :] + gin[:NP, :]
@@ -230,6 +234,8 @@
 
     for d in range(1, 4):
         send_gram(d).start()
+    pt_copy = pltpu.make_async_copy(pt, pt_out, osem)
+    pt_copy.start()
     product(NCH - 1, 2, 4)
 
     scopy = remote(part.at[:, 1 - core], rin, r1sem.at[0], r1sem.at[1], {'pr': twin})
@@ -279,7 +285,7 @@
     for d in range(1, 4):
         src = lax.rem(chip + 4 - d, 4)
         remote(part2.at[src], rsum.at[src], r2send.at[d], r2recv.at[src], {'pr': twin}).wait_recv()
-    st[me] = ((rsum[0] + rsum[1]) + rsum[2]) + rsum[3]
+    st[pl.ds(pl.multiple_of(me * OWN, 8), OWN), :] = ((rsum[0] + rsum[1]) + rsum[2]) + rsum[3]
     gather_start(st, sasend, sarecv)
     factor_steps(h_s, b_s, r_s, u_s, NB, 64, 120)
     gather_forward(st, sasend, sarecv)
@@ -299,12 +305,12 @@
     rinv = upper_inv(rmat)
     uinv = upper_inv(umat)
     linv = unit_tri_inv(-lstrict, eye)
-    wt_out[...] = (uinv * n_col).T
+    out[AUX0:, WT0:WT0 + NP] = (uinv * n_col).T
     linv_t = linv.T
     m2_t = (fdot(linv, rinv.T) * n_row).T
-    tau_out[...] = jnp.sum(jnp.where(eyeb, -umat / rmat, 0.0), axis=0, keepdims=True)
-    tops_out[:NP, :] = lmat.T
-    tops_out[NP:, :] = jnp.where(row_id > col_id, lmat, rmat * (g_row * n_row)).T
+    out[AUX0:AUX0 + 8, TAU0:TAU0 + NP] = jnp.broadcast_to(jnp.sum(jnp.where(eyeb, -umat / rmat, 0.0), axis=0, keepdims=True), (8, NP))
+    out[AUX0:, TOP0:TOP0 + NP] = lmat.T
+    out[AUX0:, TOP1:TOP1 + NP] = jnp.where(row_id > col_id, lmat, rmat * (g_row * n_row)).T
 
     mcopy.wait()
     c_top = jnp.max(jnp.maximum(cmx[0], cmx[1]), axis=1, keepdims=True)[:1]
@@ -318,19 +324,20 @@
     cond = total_of(rinv * rinv + uinv * uinv + linv * linv)
     good = (g_max < 1e12) & (g_min > 1e-12) & (resid < 1e-3) & (cond < 2048.0)
     good = good & (c_top < 1e26) & ((c_top > 1e-20) | (c_top == 0.0))
-    bad_out[...] = jnp.broadcast_to(jnp.where(good, 0.0, 1.0), (8, NP))
+    out[AUX0:AUX0 + 8, BAD0:BAD0 + NP] = jnp.broadcast_to(jnp.where(good, 0.0, 1.0), (8, NP))
 
     gather_wait(st, sasend, sarecv)
 
-    def make_z(i, carry):
-        zt_out[pl.ds(pl.multiple_of(i * OWN, OWN), OWN), :] = fdot(ct[i], linv_t) - fdot(st[i], m2_t)
-        return carry
-
-    lax.fori_loop(0, NPR, make_z, 0)
-
-    pt_copy.wait()
+    for b in range(4):
+        rows = slice(b * MROWS, (b + 1) * MROWS)
+        zpart[rows, :] = fdot(ct[rows, :], linv_t) - fdot(st[rows, :], m2_t)
+    for b in range(16):
+        n = min(NP, TRAIL - b * NP)
+        out[AUX0:AUX0 + n, b * NP:(b + 1) * NP] = zpart[b * NP:b * NP + n, :]
+
     for c in range(NCH):
         send_panel(c).wait_send()
+    pt_copy.wait()
     gather_end(ct, casend, carecv)
     gather_end(st, sasend, sarecv)
     for d in range(1, 4):
@@ -351,70 +358,112 @@
     hbm = pl.BlockSpec(memory_space=pl.ANY)
     return pl.pallas_call(
         reduce_kernel,
-        out_shape=(
-            jax.ShapeDtypeStruct((NP, ROWS), f32), jax.ShapeDtypeStruct((NP, NP), f32), jax.ShapeDtypeStruct((TRAIL, NP), f32),
-            jax.ShapeDtypeStruct((2 * NP, NP), f32), jax.ShapeDtypeStruct((1, NP), f32), jax.ShapeDtypeStruct((8, NP), f32)),
+        out_shape=(pltpu.VMEM((ALL, ROWS), f32), pltpu.HBM((NP, ROWS), f32)),
         in_specs=[hbm, hbm],
-        out_specs=(hbm, vmem, vmem, vmem, vmem, vmem),
+        out_specs=(vmem, hbm),
         scratch_shapes=[
-            pltpu.VMEM((TRAIL, ROWS), f32), pltpu.VMEM((NP, ROWS), f32), pltpu.VMEM((LANES, 3 * NP), jnp.bfloat16),
+            pltpu.VMEM((NP, ROWS), f32), pltpu.VMEM((LANES, 3 * NP), jnp.bfloat16),
             pltpu.VMEM((MSG, NP), f32), pltpu.VMEM((MSG, NP), f32), pltpu.VMEM((4, MSG, NP), f32), pltpu.VMEM((NP, NP), f32),
-            pltpu.VMEM((NPR, OWN, NP), f32), pltpu.VMEM((4, 2, OWN, NP), f32), pltpu.VMEM((4, OWN, NP), f32), pltpu.VMEM((4, OWN, NP), f32),
-            pltpu.VMEM((4, OWN, NP), f32), pltpu.VMEM((NPR, OWN, NP), f32),
+            pltpu.VMEM((TRAIL, NP), f32), pltpu.VMEM((4, 2, OWN, NP), f32), pltpu.VMEM((4, OWN, NP), f32), pltpu.VMEM((4, OWN, NP), f32),
+            pltpu.VMEM((4, OWN, NP), f32), pltpu.VMEM((TRAIL, NP), f32), pltpu.VMEM((TRAIL, NP), f32),
             pltpu.VMEM((NP, NP), f32), pltpu.VMEM((NP, NP), f32), pltpu.VMEM((NP, NP), f32), pltpu.VMEM((NP, NP), f32), pltpu.VMEM((2, 8, NP), f32),
             dma((NCH,)), dma((NCH,)), dma((NCH,)), dma((NCH,)), dma(()), dma((4,)), dma((5,)), dma((NPR,)), dma(()), dma((NPR,)), dma(()),
             dma((2,)), dma((4,)), dma((4,)), dma((7,)), dma((NPR,)), dma((7,)), dma((NPR,)), dma((2,))],
-        compiler_params=pltpu.CompilerParams(collective_id=0, has_side_effects=True, vmem_limit_bytes=67043328),
+        compiler_params=pltpu.CompilerParams(collective_id=0, has_side_effects=True, vmem_limit_bytes=18 << 20),
         name='reduce',
-    )(panel_t, trail_t)
+    )(pltpu.with_memory_space_constraint(panel_t, pltpu.HBM), pltpu.with_memory_space_constraint(trail_t, pltpu.HBM))
 
 
 UL = 512
-
-
-def update_kernel(pt_ref, wt_ref, zt_ref, tops_ref, c_ref, o_ref, pan_ref, zcat, vcat):
-    first = pl.program_id(0) == 0
+NUL = ROWS // UL
+
+
+def update_kernel(c_ref, pt_hbm, o_hbm, pan_hbm, tau_out, bad_out, pt, zcat, va, vb, sa, sb, pan, osem, psem, isem):
     q = lax.axis_index('pc')
-
-    @pl.when(first)
-    def _():
-        zh, zm, zl = split3(zt_ref[...])
+    head = pltpu.make_async_copy(pt_hbm.at[:, :UL], pt.at[:, :UL], isem.at[0])
+    tail = pltpu.make_async_copy(pt_hbm.at[:, UL:], pt.at[:, UL:], isem.at[1])
+    head.start()
+    tail.start()
+    for b in range(16):
+        rows = min(NP, TRAIL - b * NP)
+        zh, zm, zl = split3(c_ref[AUX0:AUX0 + rows, b * NP:(b + 1) * NP])
         for n, piece in enumerate((zh, zh, zm, zm, zl, zh)):
-            zcat[:, n * NP:(n + 1) * NP] = piece
-
-    v = fdot(wt_ref[...], pt_ref[...])
-    at_top = first & (lax.axis_index('pr') == 0)
-    lane = lax.broadcasted_iota(jnp.int32, (NP, UL), 1)
-    inside = (lane < NP) & at_top
-    pad = jnp.zeros((NP, UL - NP), jnp.float32)
-    stored = jnp.where(inside, jnp.concatenate([tops_ref[NP:, :], pad], axis=1), v)
-    v = jnp.where(inside, jnp.concatenate([tops_ref[:NP, :], pad], axis=1), v)
-    pan_ref[...] = jnp.where(q == 0, stored[:NB], stored[NB:])
-    vh, vm, vl = split3(v)
-    for n, piece in enumerate((vh, vm, vh, vm, vh, vl)):
-        vcat[n * NP:(n + 1) * NP, :] = piece
-
-    def rows_step(m, carry):
-        rows = pl.ds(pl.multiple_of(m * MROWS, MROWS), MROWS)
-        o_ref[rows, :] = c_ref[rows, :] - bdot(zcat[rows, :], vcat[...])
+            zcat[b * NP:b * NP + rows, n * NP:(n + 1) * NP] = piece
+    tau_out[...] = c_ref[AUX0:AUX0 + 1, TAU0:TAU0 + NP]
+    bad_out[...] = c_ref[AUX0:AUX0 + 1, BAD0:BAD0 + NP]
+
+    def tile(i):
+        return pl.ds(pl.multiple_of(i * UL, UL), UL)
+
+    def make_v(i, vcat, first=False):
+        v = fdot(c_ref[AUX0:, WT0:WT0 + NP], pt[:, tile(i)])
+        stored = v
+        if first:
+            inside = (lax.broadcasted_iota(jnp.int32, (NP, UL), 1) < NP) & (lax.axis_index('pr') == 0)
+            pad = jnp.zeros((NP, UL - NP), jnp.float32)
+            stored = jnp.where(inside, jnp.concatenate([c_ref[AUX0:, TOP1:TOP1 + NP], pad], axis=1), v)
+            v = jnp.where(inside, jnp.concatenate([c_ref[AUX0:, TOP0:TOP0 + NP], pad], axis=1), v)
+        pan[:, tile(i)] = jnp.where(q == 0, stored[:NB], stored[NB:])
+        vh, vm, vl = split3(v)
+        for n, piece in enumerate((vh, vm, vh, vm, vh, vl)):
+            vcat[n * NP:(n + 1) * NP, :] = piece
+
+    def make_out(i, vcat, stage):
+        for m in range(TRAIL // MROWS):
+            rows = slice(m * MROWS, (m + 1) * MROWS)
+            stage[rows, :] = c_ref[rows, tile(i)] - bdot(zcat[rows, :], vcat[...])
+
+    def put(i, stage, k):
+        return pltpu.make_async_copy(stage, o_hbm.at[:, tile(i)], osem.at[k])
+
+    head.wait()
+    make_v(0, va, True)
+    tail.wait()
+
+    def pair(p, carry):
+        i = 2 * p
+
+        @pl.when(p > 0)
+        def _():
+            put(i, sa, 0).wait()
+
+        make_v(i + 1, vb)
+        make_out(i, va, sa)
+        put(i, sa, 0).start()
+
+        @pl.when(p > 0)
+        def _():
+            put(i, sb, 1).wait()
+
+        make_v(jnp.minimum(i + 2, NUL - 1), va)
+        make_out(i + 1, vb, sb)
+        put(i + 1, sb, 1).start()
         return carry
 
-    lax.fori_loop(0, TRAIL // MROWS, rows_step, 0)
-
-
-def update_call(pt, wt, zt, tops, trail_t):
+    lax.fori_loop(0, NUL // 2, pair, 0)
+    pan_copy = pltpu.make_async_copy(pan, pan_hbm, psem)
+    pan_copy.start()
+    put(0, sa, 0).wait()
+    put(0, sb, 1).wait()
+    pan_copy.wait()
+
+
+def update_call(work, pt):
     f32 = jnp.float32
+    vmem = pl.BlockSpec(memory_space=pltpu.VMEM)
+    hbm = pl.BlockSpec(memory_space=pl.ANY)
     return pl.pallas_call(
         update_kernel,
-        out_shape=(jax.ShapeDtypeStruct((TRAIL, ROWS), f32), jax.ShapeDtypeStruct((NB, ROWS), f32)),
-        grid=(ROWS // UL,),
-        in_specs=[pl.BlockSpec((NP, UL), lambda i: (0, i)), pl.BlockSpec((NP, NP), lambda i: (0, 0)), pl.BlockSpec((TRAIL, NP), lambda i: (0, 0)),
-                  pl.BlockSpec((2 * NP, NP), lambda i: (0, 0)), pl.BlockSpec((TRAIL, UL), lambda i: (0, i))],
-        out_specs=(pl.BlockSpec((TRAIL, UL), lambda i: (0, i)), pl.BlockSpec((NB, UL), lambda i: (0, i))),
-        scratch_shapes=[pltpu.VMEM((TRAIL, 6 * NP), jnp.bfloat16), pltpu.VMEM((6 * NP, UL), jnp.bfloat16)],
-        compiler_params=pltpu.CompilerParams(dimension_semantics=('arbitrary',), vmem_limit_bytes=40 << 20),
+        out_shape=(jax.ShapeDtypeStruct((TRAIL, ROWS), f32), jax.ShapeDtypeStruct((NB, ROWS), f32), jax.ShapeDtypeStruct((1, NP), f32), jax.ShapeDtypeStruct((1, NP), f32)),
+        in_specs=[vmem, hbm],
+        out_specs=(hbm, hbm, vmem, vmem),
+        scratch_shapes=[
+            pltpu.VMEM((NP, ROWS), f32), pltpu.VMEM((TRAIL, 6 * NP), jnp.bfloat16), pltpu.VMEM((6 * NP, UL), jnp.bfloat16), pltpu.VMEM((6 * NP, UL), jnp.bfloat16),
+            pltpu.VMEM((TRAIL, UL), f32), pltpu.VMEM((TRAIL, UL), f32), pltpu.VMEM((NB, ROWS), f32),
+            pltpu.SemaphoreType.DMA((2,)), pltpu.SemaphoreType.DMA(()), pltpu.SemaphoreType.DMA((2,))],
+        compiler_params=pltpu.CompilerParams(vmem_limit_bytes=20 << 20),
         name='update',
-    )(pt, wt, zt, tops, trail_t)
+    )(work, pltpu.with_memory_space_constraint(pt, pltpu.HBM))
 
 
 def sum_rows(x):
@@ -465,10 +514,10 @@
     return lax.fori_loop(0, NB, t_step, jnp.zeros((NB, NB), jnp.float32))
 
 
-def by_columns(panel, trail):
+def by_columns(panel, trail, shift):
     col_idx = lax.axis_index('pc')
-    row_ids = lax.axis_index('pr') * ROWS + jnp.arange(ROWS)
-    v_parts, z_parts, taus = [], [], []
+    row_ids = lax.axis_index('pr') * ROWS + jnp.arange(ROWS) + shift
+    taus = []
     for k in range(2):
         fac_panel, tau_vec = factor_panel(panel, row_ids, k * NB)
         diag = k * NB + jnp.arange(NB)
@@ -476,37 +525,29 @@
         v_mat = from_owner(v_mat, k)
         tau_vec = from_owner(tau_vec, k)
         t_mat = build_t(sum_rows(mat_prod('rb,rc->bc', v_mat, v_mat)), tau_vec)
-        inner = mat_prod('bd,bc->dc', t_mat, sum_rows(mat_prod('rb,rc->bc', v_mat, trail)))
-        if k == 0:
-            trail = trail - mat_prod('rd,dc->rc', v_mat, inner)
-            near = mat_prod('bd,bc->dc', t_mat, sum_rows(mat_prod('rb,rc->bc', v_mat, panel)))
-            later = panel - mat_prod('rd,dc->rc', v_mat, near)
-            panel = jnp.where(col_idx == 0, fac_panel, later)
-        else:
-            panel = jnp.where(col_idx == 1, fac_panel, panel)
-        v_parts.append(v_mat)
-        z_parts.append(inner)
+
+        def updated(cols):
+            inner = mat_prod('bd,bc->dc', t_mat, sum_rows(mat_prod('rb,rc->bc', v_mat, cols)))
+            return cols - mat_prod('rd,dc->rc', v_mat, inner)
+
+        trail = updated(trail)
+        later = updated(panel) if k == 0 else panel
+        panel = jnp.where(col_idx == k, fac_panel, later)
         taus.append(tau_vec)
-    v_t = jnp.concatenate(v_parts, axis=1).T
-    top = panel[:NP].T
-    tops = jnp.concatenate([v_t[:, :NP], top, top], axis=0)
-    return v_t, jnp.eye(NP, dtype=jnp.float32), jnp.concatenate(z_parts, axis=0).T, tops, jnp.concatenate(taus)[None, :]
+    return trail.T, panel.T, jnp.concatenate(taus)[None, :]
 
 
 def solution(mesh):
     def local_run(panels_loc, trail_loc):
         panel_t = panels_loc.reshape(ROWS, NB).T
         trail_t = trail_loc.T
-        pt, wt, zt, tops, tau, bad = reduce_call(panel_t, trail_t)
-
-        def direct(pt, wt, zt, tops, tau, trail_t, panel_t):
-            return update_call(pt, wt, zt, tops, trail_t) + (tau,)
-
-        def again(pt, wt, zt, tops, tau, trail_t, panel_t):
-            pt, wt, zt, tops, tau = by_columns(panel_t.T, trail_t.T)
-            return update_call(pt, wt, zt, tops, trail_t) + (tau,)
-
-        trail_new, pan, tau = lax.cond(bad[0, 0] > 0.0, again, direct, pt, wt, zt, tops, tau, trail_t, panel_t)
+        trail_new, pan, tau, bad = update_call(*reduce_call(panel_t, trail_t))
+
+        def again(state):
+            shift = (state[0][0, 0] < 0.0).astype(jnp.int32)
+            return (jnp.zeros_like(state[0]),) + by_columns(panel_t.T, trail_t.T, shift)
+
+        _, trail_new, pan, tau = lax.while_loop(lambda s: s[0][0, 0] > 0.0, again, (bad, trail_new, pan, tau))
         return pan.T.reshape(ROWS, 1, NB), trail_new.T, tau.reshape(NP)
 
     return jax.shard_map(local_run, mesh=mesh, in_specs=(P('pr', 'pc', None), P('pr', 'pc')), out_specs=(P('pr', 'pc', None), P('pr', 'pc'), P()), check_vma=False)

time: 100 us -> 83.7 us (0.84)
  Pallas kernels: 95.9 us -> 81.8 us
  local copies, waits for them, and re-layouts: 2.33 us -> 0.01 us
    pallas_call x1, Pallas kernels: 30.6 us -> 19.8 us  [update_call(): pl.pallas_call(update_kernel, out_shape=(jax.ShapeDtypeStruct((TRAIL, ROW...]
    pallas_call x1, Pallas kernels: 65.4 us -> 62 us  [reduce_call(): pl.pallas_call(reduce_kernel, out_shape=(pltpu.VMEM((ALL, ROWS), f32), pl...]
    slice x1 -> x0, local copies, waits for them, and re-layouts: 1.19 us -> none  [local_run(): bad[0, 0] > 0.0]
    unnamed x1 -> x2, local copies, waits for them, and re-layouts: 1.14 us -> 0.01 us
where the time goes in v2:
time: 83.7 us; the launch traced here: 83.5 us
  Pallas kernels  81.8 us (98%)
  loops' own time  0.85 us (1%)
  between operations  0.84 us (1%)
    pallas_call x1, Pallas kernels, reduce_call(): pl.pallas_call(reduce_kernel, out_shape=(pltpu.VMEM((ALL, ROWS), f32), pl...  62 us
    pallas_call x1, Pallas kernels, update_call(): pl.pallas_call(update_kernel, out_shape=(jax.ShapeDtypeStruct((TRAIL, ROW...  19.8 us

profile of v2, /device:TPU:0, one launch (start us, length us, event | category | flops | bytes accessed | tf_op | source)
XLA Modules:
  0.0 83.5 jit_solution(17686645349043770604)
XLA Ops:
  0.6 0.0 copy-start
  0.6 62.0 %reduce.1 = (f32[2112,4096]{1,0:T(8,128)S(1)}, f32[128,4096]{1,0:T(8,128)}) custom-call(f32[64,4096]{1,0:T(8,128)} %bitcast.139, f32[1984,4096]{1,0:T(8,128)} %bitcast.138), custom_call_target="tpu_custom_call" | custom-call | tf_op jit(solution)/shard_map/reduce/pallas_call | solution.py:359
  62.7 19.8 %update.1 = (f32[1984,4096]{1,0:T(8,128)}, f32[64,4096]{1,0:T(8,128)}, f32[1,128]{1,0:T(1,128)}, f32[1,128]{1,0:T(1,128)}) custom-call(f32[2112,4096]{1,0:T(8,128)S(1)} %get-tuple-element.430.c_ref, f32[128,4096]{1,0:T(8,128)} %get-tuple-element.431.pt_hbm), custom_call_target="tpu_custom_call" | custom-call | tf_op jit(solution)/shard_map/update/pallas_call | solution.py:455
  82.5 0.0 copy-done
  82.5 0.8 %while.82 = (f32[1,128]{1,0:T(1,128)}, f32[1984,4096]{1,0:T(8,128)}, f32[64,4096]{1,0:T(8,128)}, f32[1,128]{1,0:T(1,128)}, f32[4096,64]{0,1:T(8,128)S(1)}, /*ind...) while((f32[1,128]{1,0:T(1,128)}, ...), condition=%wide.region_19.20_spmd, body=%wide.region_0.19_spmd.sunk | while | flops 25993101312 | bytes 270397856 | solution.py:550
Async XLA Ops:
  0.6 81.9 %copy-start = (f32[4096,1,64]{0,2,1:T(8,128)S(1)}, f32[4096,1,64]{0,2,1:T(8,128)}, u32[]{:S(2)}) copy-start(f32[4096,1,64]{0,2,1:T(8,128)} %param.12) | copy-start | bytes 3145732

commit v3 on v2

--- a/solution.py
+++ b/solution.py
@@ -9,8 +9,9 @@
 MESH = pl.DeviceIdType.MESH
 ROWS, NB, NP, TRAIL = 4096, 64, 128, 1984
 NPR = 8
+CHUNKS = ((0, 1024), (1024, 1024), (2048, 1024), (3072, 512), (3584, 512))
 LANES = 1024
-NCH = ROWS // LANES
+NCH = len(CHUNKS)
 AUX0, ALL = TRAIL, TRAIL + NP
 WT0, TOP0, TOP1, TAU0, BAD0 = (16 * NP, 17 * NP, 18 * NP, 19 * NP, 20 * NP)
 OWN = TRAIL // NPR
@@ -47,32 +48,37 @@
 
 
 def unit_tri_inv(strict, eye):
+    n = strict.shape[0]
     inv = eye + strict
-    power = strict
-    for _ in range(6):
-        power = fdot(power, power)
-        inv = inv + fdot(inv, power)
-    return inv
+    power = fdot(strict, strict)
+    for _ in range(5):
+        both = dot_parts(jnp.concatenate([inv, power], axis=0), jnp.concatenate(split3(power), axis=1))
+        inv = inv + both[:n]
+        power = both[n:]
+    return inv + fdot(inv, power)
 
 
 def eye_of(n):
     return lax.broadcasted_iota(jnp.int32, (n, n), 0) == lax.broadcasted_iota(jnp.int32, (n, n), 1)
 
 
-def factor_steps(h_s, b_s, r_s, u_s, row0, start, stop):
-    n_rows = NP - row0
+def column_of(ref, row0, j):
+    return jnp.take_along_axis(ref[row0:, :], jnp.full((NP - row0, NP), j, jnp.int32), axis=1)
+
+
+def factor_steps(h_s, b_s, r_s, u_s, hc_s, bc_s, bn_s, row0, start, stop):
     lane1 = lax.broadcasted_iota(jnp.int32, (1, NP), 1)
-    lane = lax.broadcasted_iota(jnp.int32, (n_rows, NP), 1)
+    lane = lax.broadcasted_iota(jnp.int32, (NP - row0, NP), 1)
 
     def step(j, carry):
-        idx = jnp.full((n_rows, NP), j, jnp.int32)
-        idx8 = jnp.full((8, NP), j, jnp.int32)
-        hrow = h_s[pl.ds(j, 1), :]
-        brow = b_s[pl.ds(j, 1), :]
-        hjj = jnp.take_along_axis(jnp.broadcast_to(hrow, (8, NP)), idx8, axis=1)[:1]
-        alpha = jnp.take_along_axis(jnp.broadcast_to(brow, (8, NP)), idx8, axis=1)[:1]
-        hcol = jnp.take_along_axis(h_s[row0:, :], idx, axis=1)
-        bcol = jnp.take_along_axis(b_s[row0:, :], idx, axis=1)
+        after = jnp.minimum(j + 1, NP - 1)
+        hnext = column_of(h_s, row0, after)
+        bnext = column_of(b_s, row0, after)
+        bn_s[row0:, :] = bnext
+        hcol, bcol = hc_s[row0:, :], bc_s[row0:, :]
+        hjj, alpha = hc_s[pl.ds(j, 1), :], bc_s[pl.ds(j, 1), :]
+        hjn, bjn = hc_s[pl.ds(after, 1), :], bn_s[pl.ds(j, 1), :]
+        hrow, brow = h_s[pl.ds(j, 1), :], b_s[pl.ds(j, 1), :]
         root = lax.rsqrt(hjj)
         root = root * (1.5 - 0.5 * hjj * root * root)
         beta = jnp.where(alpha >= 0.0, -hjj * root, hjj * root)
@@ -83,16 +89,23 @@
         urow = jnp.where(keep, brow - rrow, 0.0)
         r_s[pl.ds(j, 1), :] = rrow
         u_s[pl.ds(j, 1), :] = urow
+        vcol = bcol * invd
+        hc_s[row0:, :] = hnext - hcol * (hjn * invb * invb)
+        bc_s[row0:, :] = bnext - vcol * (bjn - hjn * invb)
         h_s[row0:, :] = h_s[row0:, :] - hcol * (rrow * invb)
-        vcol = bcol * invd
         b_s[row0:, :] = jnp.where(lane == j, vcol, b_s[row0:, :] - vcol * urow)
         return carry
 
-    lax.fori_loop(start, stop, step, 0)
+    def four(g, carry):
+        for i in range(4):
+            step(start + 4 * g + i, carry)
+        return carry
+
+    lax.fori_loop(0, (stop - start) // 4, four, 0)
 
 
 def reduce_kernel(panel_hbm, trail_hbm, out, pt_out,
-                  pt, pp, gown, gin, gsum, ptop, ct, part, rin, part2, rsum, st, zpart, h_s, b_s, r_s, u_s, cmx,
+                  pt, pp, gown, gin, gsum, ptop, ct, part, rin, part2, rsum, st, zpart, h_s, b_s, r_s, u_s, hc_s, bc_s, bn_s, cmx,
                   csem, psem, zsend, zrecv, osem, gsend, grecv, tsend, trecv, csend, crecv, r1sem, r2send, r2recv,
                   casend, carecv, sasend, sarecv, msem):
     cbuf = out.at[pl.ds(0, TRAIL), :]
@@ -109,7 +122,7 @@
         return pltpu.make_async_remote_copy(src_ref=src, dst_ref=dst, send_sem=s_sem, recv_sem=r_sem, device_id=dev, device_id_type=MESH)
 
     def lanes(c):
-        return pl.ds(c * LANES, LANES)
+        return pl.ds(*CHUNKS[c])
 
     def load_trail(c):
         return pltpu.make_async_copy(trail_hbm.at[:, lanes(c)], cbuf.at[:, lanes(c)], csem.at[c])
@@ -170,22 +183,23 @@
     gown[...] = jnp.zeros_like(gown)
 
     def make_pieces(c):
+        n = CHUNKS[c][1]
         hi, mid, low = split3(pt[:, lanes(c)].T)
-        pp[:, :NP] = hi
-        pp[:, NP:2 * NP] = mid
-        pp[:, 2 * NP:] = low
-        gown[:NP, :] += dot_parts(pt[:, lanes(c)], pp[...])
+        pp[:n, :NP] = hi
+        pp[:n, NP:2 * NP] = mid
+        pp[:n, 2 * NP:] = low
+        gown[:NP, :] += dot_parts(pt[:, lanes(c)], pp[:n, :])
 
     def product(c, first, last):
         def rows_step(m, carry):
             rows = pl.ds(pl.multiple_of(m * MROWS, MROWS), MROWS)
-            got = dot_parts(cbuf[rows, lanes(c)], pp[...])
+            got = dot_parts(cbuf[rows, lanes(c)], pp[:CHUNKS[c][1], :])
             part[m] += got.reshape(2, OWN, NP)
             return carry
 
         lax.fori_loop(first, last, rows_step, 0)
 
-    cmax = jnp.zeros((8, LANES), jnp.float32)
+    cmax = jnp.zeros((8, 1), jnp.float32)
     for c in range(NCH):
         load_trail(c).wait()
         if c == 0:
@@ -197,9 +211,10 @@
 
         def largest(m, acc):
             x = cbuf[pl.ds(pl.multiple_of(m * OWN, OWN), OWN), lanes(c)]
-            return jnp.maximum(acc, jnp.max(jnp.abs(x).reshape(OWN // 8, 8, LANES), axis=0))
-
-        cmax = lax.fori_loop(0, NPR, largest, cmax)
+            return jnp.maximum(acc, jnp.max(jnp.abs(x).reshape(OWN // 8, 8, CHUNKS[c][1]), axis=0))
+
+        most = lax.fori_loop(0, NPR, largest, jnp.zeros((8, CHUNKS[c][1]), jnp.float32))
+        cmax = jnp.maximum(cmax, jnp.max(most, axis=1, keepdims=True))
         if c == 1:
             @pl.when(me != 0)
             def _():
@@ -219,7 +234,7 @@
         if c < NCH - 1:
             product(c, 0, 4)
 
-    big = jnp.max(jnp.max(cmax, axis=1, keepdims=True), axis=0, keepdims=True)
+    big = jnp.max(cmax, axis=0, keepdims=True)
     gown[NP:, :] = jnp.broadcast_to(big, (8, NP))
 
     gcopy = remote(gown, gin, gsend.at[0], grecv.at[4], {'pr': twin})
@@ -240,6 +255,18 @@
 
     scopy = remote(part.at[:, 1 - core], rin, r1sem.at[0], r1sem.at[1], {'pr': twin})
     scopy.start()
+    scopy.wait()
+    for s in range(4):
+        part2[s] = part[s, core] + rin[s]
+
+    def scatter_part(d):
+        to = lax.rem(chip + d, 4)
+        return remote(part2.at[to], rsum.at[chip], r2send.at[d], r2recv.at[chip], {'pr': 2 * to + core})
+
+    for d in range(1, 4):
+        send_gram(d).wait_send()
+    for d in range(1, 4):
+        scatter_part(d).start()
 
     @pl.when(me != 0)
     def _():
@@ -268,29 +295,17 @@
     n_row, n_col = newton_rsqrt(g_row), newton_rsqrt(g_col)
     h_s[...] = (gram * n_row) * n_col
     b_s[...] = ptop[...].T * n_row
-    factor_steps(h_s, b_s, r_s, u_s, 0, 0, 16)
-
-    scopy.wait()
-    for s in range(4):
-        part2[s] = part[s, core] + rin[s]
-
-    def scatter_part(d):
-        to = lax.rem(chip + d, 4)
-        return remote(part2.at[to], rsum.at[chip], r2send.at[d], r2recv.at[chip], {'pr': 2 * to + core})
-
-    for d in range(1, 4):
-        scatter_part(d).start()
-    factor_steps(h_s, b_s, r_s, u_s, 0, 16, 64)
+    hc_s[...] = column_of(h_s, 0, 0)
+    bc_s[...] = column_of(b_s, 0, 0)
+    factor_steps(h_s, b_s, r_s, u_s, hc_s, bc_s, bn_s, 0, 0, 64)
     rsum[chip] = part2[chip]
     for d in range(1, 4):
         src = lax.rem(chip + 4 - d, 4)
         remote(part2.at[src], rsum.at[src], r2send.at[d], r2recv.at[src], {'pr': twin}).wait_recv()
     st[pl.ds(pl.multiple_of(me * OWN, 8), OWN), :] = ((rsum[0] + rsum[1]) + rsum[2]) + rsum[3]
     gather_start(st, sasend, sarecv)
-    factor_steps(h_s, b_s, r_s, u_s, NB, 64, 120)
-    gather_forward(st, sasend, sarecv)
+    factor_steps(h_s, b_s, r_s, u_s, hc_s, bc_s, bn_s, NB, 64, 128)
     gather_wait(ct, casend, carecv)
-    factor_steps(h_s, b_s, r_s, u_s, NB, 120, 128)
 
     rmat, umat = r_s[...], u_s[...]
     lstrict = jnp.where(row_id > col_id, b_s[...], 0.0)
@@ -312,6 +327,13 @@
     out[AUX0:, TOP0:TOP0 + NP] = lmat.T
     out[AUX0:, TOP1:TOP1 + NP] = jnp.where(row_id > col_id, lmat, rmat * (g_row * n_row)).T
 
+    linv_pieces = jnp.concatenate(split3(linv_t), axis=1)
+    m2_pieces = jnp.concatenate(split3(m2_t), axis=1)
+    gather_forward(st, sasend, sarecv)
+    for b in range(4):
+        rows = slice(b * MROWS, (b + 1) * MROWS)
+        zpart[rows, :] = dot_parts(ct[rows, :], linv_pieces)
+
     mcopy.wait()
     c_top = jnp.max(jnp.maximum(cmx[0], cmx[1]), axis=1, keepdims=True)[:1]
     g_max = jnp.max(g_row, axis=1, keepdims=True)
@@ -330,7 +352,7 @@
 
     for b in range(4):
         rows = slice(b * MROWS, (b + 1) * MROWS)
-        zpart[rows, :] = fdot(ct[rows, :], linv_t) - fdot(st[rows, :], m2_t)
+        zpart[rows, :] -= dot_parts(st[rows, :], m2_pieces)
     for b in range(16):
         n = min(NP, TRAIL - b * NP)
         out[AUX0:AUX0 + n, b * NP:(b + 1) * NP] = zpart[b * NP:b * NP + n, :]
@@ -341,7 +363,6 @@
     gather_end(ct, casend, carecv)
     gather_end(st, sasend, sarecv)
     for d in range(1, 4):
-        send_gram(d).wait_send()
         scatter_part(d).wait_send()
 
     @pl.when(me == 0)
@@ -366,7 +387,7 @@
             pltpu.VMEM((MSG, NP), f32), pltpu.VMEM((MSG, NP), f32), pltpu.VMEM((4, MSG, NP), f32), pltpu.VMEM((NP, NP), f32),
             pltpu.VMEM((TRAIL, NP), f32), pltpu.VMEM((4, 2, OWN, NP), f32), pltpu.VMEM((4, OWN, NP), f32), pltpu.VMEM((4, OWN, NP), f32),
             pltpu.VMEM((4, OWN, NP), f32), pltpu.VMEM((TRAIL, NP), f32), pltpu.VMEM((TRAIL, NP), f32),
-            pltpu.VMEM((NP, NP), f32), pltpu.VMEM((NP, NP), f32), pltpu.VMEM((NP, NP), f32), pltpu.VMEM((NP, NP), f32), pltpu.VMEM((2, 8, NP), f32),
+            pltpu.VMEM((NP, NP), f32), pltpu.VMEM((NP, NP), f32), pltpu.VMEM((NP, NP), f32), pltpu.VMEM((NP, NP), f32), pltpu.VMEM((NP, NP), f32), pltpu.VMEM((NP, NP), f32), pltpu.VMEM((NP, NP), f32), pltpu.VMEM((2, 8, NP), f32),
             dma((NCH,)), dma((NCH,)), dma((NCH,)), dma((NCH,)), dma(()), dma((4,)), dma((5,)), dma((NPR,)), dma(()), dma((NPR,)), dma(()),
             dma((2,)), dma((4,)), dma((4,)), dma((7,)), dma((NPR,)), dma((7,)), dma((NPR,)), dma((2,))],
         compiler_params=pltpu.CompilerParams(collective_id=0, has_side_effects=True, vmem_limit_bytes=18 << 20),

time: 83.7 us -> 82.8 us (0.989)
  Pallas kernels: 81.8 us -> 80.9 us
    pallas_call x1, Pallas kernels: 62 us -> 61.1 us  [reduce_call(): pl.pallas_call(reduce_kernel, out_shape=(pltpu.VMEM((ALL, ROWS), f32), pl...]
where the time goes in v3:
time: 82.8 us; the launch traced here: 82.6 us
  Pallas kernels  80.9 us (98%)
  loops' own time  0.85 us (1%)
  between operations  0.84 us (1%)
    pallas_call x1, Pallas kernels, reduce_call(): pl.pallas_call(reduce_kernel, out_shape=(pltpu.VMEM((ALL, ROWS), f32), pl...  61.1 us
    pallas_call x1, Pallas kernels, update_call(): pl.pallas_call(update_kernel, out_shape=(jax.ShapeDtypeStruct((TRAIL, ROW...  19.8 us

profile of v3, /device:TPU:0, one launch (start us, length us, event | category | flops | bytes accessed | tf_op | source)
XLA Modules:
  0.0 82.6 jit_solution(4095880488857481406)
XLA Ops:
  0.6 0.0 copy-start
  0.6 61.1 %reduce.1 = (f32[2112,4096]{1,0:T(8,128)S(1)}, f32[128,4096]{1,0:T(8,128)}) custom-call(f32[64,4096]{1,0:T(8,128)} %bitcast.139, f32[1984,4096]{1,0:T(8,128)} %bitcast.138), custom_call_target="tpu_custom_call" | custom-call | tf_op jit(solution)/shard_map/reduce/pallas_call | solution.py:380
  61.8 19.8 %update.1 = (f32[1984,4096]{1,0:T(8,128)}, f32[64,4096]{1,0:T(8,128)}, f32[1,128]{1,0:T(1,128)}, f32[1,128]{1,0:T(1,128)}) custom-call(f32[2112,4096]{1,0:T(8,128)S(1)} %get-tuple-element.430.c_ref, f32[128,4096]{1,0:T(8,128)} %get-tuple-element.431.pt_hbm), custom_call_target="tpu_custom_call" | custom-call | tf_op jit(solution)/shard_map/update/pallas_call | solution.py:476
  81.6 0.0 copy-done
  81.6 0.8 %while.82 = (f32[1,128]{1,0:T(1,128)}, f32[1984,4096]{1,0:T(8,128)}, f32[64,4096]{1,0:T(8,128)}, f32[1,128]{1,0:T(1,128)}, f32[4096,64]{0,1:T(8,128)S(1)}, /*ind...) while((f32[1,128]{1,0:T(1,128)}, ...), condition=%wide.region_19.20_spmd, body=%wide.region_0.19_spmd.sunk | while | flops 25993101312 | bytes 270397856 | solution.py:571
Async XLA Ops:
  0.6 81.0 %copy-start = (f32[4096,1,64]{0,2,1:T(8,128)S(1)}, f32[4096,1,64]{0,2,1:T(8,128)}, u32[]{:S(2)}) copy-start(f32[4096,1,64]{0,2,1:T(8,128)} %param.12) | copy-start | bytes 3145732
